TPU v7x, 32 devices: a whole 2x2x4 slice. The times are simulated.
32 devices in a mesh: wave: 4 (over y, x), freq: 8 (over z, core).
Axes of the slice: x: 2, y: 2, z: 4, core: 2. Of those that a mesh axis runs over, the one named last changes fastest.
Arguments:
- waveforms: float32 [1024, 16384], P('wave', 'freq'), may hold values from -6 to 6
- pivots: int32 [2, 128], replicated, may hold values from 0 to 1023, as said below
- nodes: int32 [1024], replicated, may hold values from 0 to 16383, as said below
Outputs:
- residual: float32 [1024, 16384], P('wave', 'freq')
- basis_rows: float32 [256, 16384], P(None, 'freq')
- fitted: float32 [1024, 16384], P('wave', 'freq')
Inputs may be any that keep to these rules, and one draw needn't show every extreme that they name: `pivots`: all 256 pivot indices are different. `nodes`: all node indices are different.
All inputs are finite; a program needn't handle non-finite values.
Results may differ from a plain program's by a relative error of at most 0.0001.
Values sent between devices are 32-bit elements; how exact they have to be, the bound alone decides.
A program may use at most 64 MiB of HBM per device.

v0:
```python
import jax
import jax.numpy as jnp
from jax import lax
from jax.sharding import PartitionSpec as P

HIGH = lax.Precision.HIGH


def body(waveforms, pivots, nodes):
    rows_here, cols_here = waveforms.shape
    row_start = lax.axis_index("wave") * rows_here
    col_start = lax.axis_index("freq") * cols_here
    picks = pivots.reshape(-1)
    count = picks.shape[0]
    local_rows = picks - row_start
    inside = ((local_rows >= 0) & (local_rows < rows_here)).astype(jnp.float32)
    picked = jnp.take(waveforms, jnp.clip(local_rows, 0, rows_here - 1), axis=0) * inside[:, None]
    pivot_rows = lax.psum(picked, "wave")
    columns = col_start + jnp.arange(cols_here, dtype=jnp.int32)
    node_count = jnp.sum((nodes[:, None] == columns[None, :]).astype(jnp.float32), axis=0)
    weighted = pivot_rows * node_count[None, :]
    left = jnp.concatenate([pivot_rows, waveforms], axis=0)
    right = jnp.concatenate([pivot_rows, weighted], axis=0)
    total = lax.psum(jnp.dot(left, right.T, precision=HIGH), "freq")
    gram, node_gram = (total[:count, :count], total[:count, count:])
    cross, node_cross = (total[count:, :count], total[count:, count:])
    factors = jnp.linalg.cholesky(jnp.stack([gram, node_gram]))
    eye = jnp.broadcast_to(jnp.eye(count, dtype=jnp.float32), factors.shape)
    inverses = jax.scipy.linalg.solve_triangular(factors, eye, lower=True)
    hi = lax.Precision.HIGHEST
    basis_rows = jnp.dot(inverses[0], pivot_rows, precision=HIGH)
    coeffs = jnp.dot(cross, inverses[0].T, precision=hi)
    residual = waveforms - jnp.dot(coeffs, basis_rows, precision=HIGH)
    coefficients = jnp.dot(
        jnp.dot(node_cross, inverses[1].T, precision=hi), inverses[1], precision=hi
    )
    fitted = jnp.dot(coefficients, pivot_rows, precision=HIGH)
    return (residual, basis_rows, fitted)


def solution(mesh):
    in_specs = (P("wave", "freq"), P(), P())
    out_specs = (P("wave", "freq"), P(None, "freq"), P("wave", "freq"))
    return jax.shard_map(body, mesh=mesh, in_specs=in_specs, out_specs=out_specs, check_vma=False)
```

profile of v0, /device:TPU:0, one launch (start us, length us, event | category | flops | bytes accessed | tf_op | source)
XLA Modules:
  0.0 288.0 jit_solution(7392579073697744297)
XLA Ops:
  7.2 0.7 fusion.25
  7.9 0.7 compare_and_fusion
  8.6 4.0 %gather_fusion = f32[256,2048]{1,0:T(8,128)S(1)} fusion(f32[256,2048]{1,0:T(8,128)} %param.3, s32[1024]{0:T(1024)S(1)} %pad_clamp_fusion), kind=kCustom, calls=%fused_computation | custom fusion | bytes 4195328 | tf_op jit(solution)/shard_map/jit(_take)/gather | solution.py:17
  12.6 1.6 select_multiply_fusion
  14.3 0.5 copy-done.6
  14.9 0.9 convert_reduce_fusion
  15.8 70.8 %all-reduce.4.cloned.1.call-done = f32[256,2048]{1,0:T(8,128)} async-done(((f32[256,2048]{1,0:T(8,128)}), f32[256,2048]{1,0:T(8,128)}) %all-reduce.4.cloned.1.call-update) | async-done | bytes 2097168 | tf_op jit(solution)/shard_map/psum | solution.py:18
  86.6 2.0 broadcast_multiply_fusion
  88.8 4.6 %fusion = f32[512,512]{0,1:T(8,128)} fusion(f32[256,2048]{1,0:T(8,128)S(1)} %copy-done.1, f32[256,2048]{1,0:T(8,128)S(1)} %copy-done, f32[256,2048]{1,0:T(8,128)S(1)} %broadcast_multiply_fusion), kind=kOutput, calls=%fused_computation.6 | convolution fusion | flops 3223322624 | bytes 7340032 | tf_op jit(solution)/shard_map/dot_general | solution.py:24
  93.5 59.4 %all-reduce.6.cloned.1.call-done = f32[512,512]{0,1:T(8,128)} async-done(((f32[512,512]{0,1:T(8,128)}), f32[512,512]{0,1:T(8,128)}) %all-reduce.6.cloned.1.call-update) | async-done | bytes 1048592 | tf_op jit(solution)/shard_map/psum | solution.py:24
  152.9 1.1 slice_bitcast_fusion.1
  153.9 0.8 pad_maximum_fusion.4
  154.8 1.2 copy.14
  156.1 0.8 copy-done.4
  156.9 23.6 %custom-call.17 = f32[2,128,128]{2,1,0:T(8,128)S(1)} custom-call(f32[2,128,128]{2,1,0:T(8,128)S(1)} %cholesky.122), custom_call_target="Cholesky" | custom-call | tf_op jit(solution)/shard_map/jit(cholesky)/cholesky | solution.py:27
  180.6 19.7 %custom-call.18 = f32[2,1,128,128]{2,3,1,0:T(8,128)S(1)} custom-call(f32[2,1,128,128]{3,2,1,0:T(8,128)S(1)} %select_bitcast_fusion), custom_call_target="InvertDiagBlocksLowerTriangular" | custom-call | tf_op jit(solution)/shard_map/jit(cholesky)/cholesky | solution.py:27
  200.3 1.2 constant_dynamic-update-slice_fusion.1
  201.5 1.3 convolution_subtract_fusion.2
  202.8 23.5 %custom-call.19 = f32[2,128,128]{2,1,0:T(8,128)S(1)} custom-call(f32[2,128,128]{2,1,0:T(8,128)S(1)} %convolution_subtract_fusion.2), custom_call_target="Cholesky" | custom-call | tf_op jit(solution)/shard_map/jit(cholesky)/cholesky | solution.py:27
  226.7 5.3 %while.1 = (s32[]{:T(128)}, f32[2,256,256]{2,1,0:T(8,128)S(1)}, s32[2,2]{1,0:T(2,128)S(1)}, f32[2,2,128,128]{3,2,0,1:T(8,128)}, s32[]{:T(128)}) while((s32[]{:T(128)}, f32[2,256,256]{2,1,0:T(8,128)S(1)}, s32[2,2]{1,0:T(2,128)S(1)}, f32[2,2,128,128]{3,2,0,1:T(8,128)}, s32[]{:T(128)}) %tuple.30), condition=%wide.while_cond, body=%wide.while_body.sunk | while | flops 2 | bytes 263277 | solution.py:29
  226.7 0.6 fusion.45
  227.3 2.0 bitcast_dynamic-update-slice_fusion.2
  229.3 0.6 fusion.45
  229.9 2.0 bitcast_dynamic-update-slice_fusion.2
  231.9 40.1 %custom-call.20 = f32[2,2,128,128]{2,3,1,0:T(8,128)S(1)} custom-call(f32[2,2,128,128]{3,2,1,0:T(8,128)} %bitcast.62), custom_call_target="InvertDiagBlocksLowerTriangular" | custom-call | tf_op jit(solution)/shard_map/jit(_solve_triangular)/vmap()/triangular_solve | solution.py:29
  272.1 0.4 fusion.14
  272.9 0.4 fusion.13
  273.3 0.6 fusion.7
  274.3 0.6 fusion.9
  274.9 1.2 fusion.22
  276.1 2.5 convolution_subtract_fusion
  278.7 2.5 fusion.33
  (39 shorter events, 1.8 us)
Async XLA Ops:
  7.2 79.4 %all-reduce.4.cloned.1.call-start = ((), (), s32[]{:S(2)}) async-start(), calls=%async_computation | async-start | bytes 4194304 | tf_op jit(solution)/shard_map/psum | solution.py:18
  14.2 0.7 copy-start.6
  14.2 138.6 %all-reduce.6.cloned.1.call-start = ((), (), s32[]{:S(2)}) async-start(), calls=%async_computation.1 | async-start | bytes 2097152 | tf_op jit(solution)/shard_map/psum | solution.py:24
  15.8 72.8 %copy-start = (f32[256,2048]{1,0:T(8,128)S(1)}, f32[256,2048]{1,0:T(8,128)}, u32[]{:S(2)}) copy-start(f32[256,2048]{1,0:T(8,128)} %param.3) | copy-start | bytes 6291460
  86.6 2.2 copy-start.1
  156.1 0.8 copy-start.4
  272.1 1.3 copy-start.5
  272.9 2.0 copy-start.2
  276.1 2.5 copy-start.3
Sparse Core Ops, SparseCore 0:
  14.3 72.1 all-reduce.3
  93.5 59.2 all-reduce.5
where the time goes:
time: 288 us
  waiting for transfers between devices  130 us (45%)
  other arithmetic  114 us (40%)
  matrix products  16.1 us (6%)
  between operations  14.3 us (5%)
  local copies, waits for them, and re-layouts  13.3 us (5%)
    psum x1, waiting for transfers between devices, body(): pivot_rows = lax.psum(picked, 'wave')  70.8 us
    another operation x10, other arithmetic, body(): factors = jnp.linalg.cholesky(jnp.stack([gram, node_gram]))  67.8 us
    psum x1, waiting for transfers between devices, body(): total = lax.psum(jnp.dot(left, right.T, precision=HIGH), 'freq')  59.4 us
    another operation x4, other arithmetic, body(): inverses = jax.scipy.linalg.solve_triangular(factors, eye, lower=True)  40.3 us
  transfers between devices with their start and end apart: 2, of which 2 were waited for; matrix products, arithmetic and copies ran while one was open for 0% of the time, Pallas kernels for 0%

commit v1 on v0

--- a/solution.py
+++ b/solution.py
@@ -21,7 +21,9 @@
     weighted = pivot_rows * node_count[None, :]
     left = jnp.concatenate([pivot_rows, waveforms], axis=0)
     right = jnp.concatenate([pivot_rows, weighted], axis=0)
-    total = lax.psum(jnp.dot(left, right.T, precision=HIGH), "freq")
+    x = jnp.dot(left, right.T, precision=HIGH)
+    terms = lax.all_gather(x, "freq", axis=0, tiled=False)
+    total = terms.sum(axis=0)
     gram, node_gram = (total[:count, :count], total[:count, count:])
     cross, node_cross = (total[count:, :count], total[count:, count:])
     factors = jnp.linalg.cholesky(jnp.stack([gram, node_gram]))

time: 288 us -> 337 us (1.17)
  waiting for transfers between devices: 130 us -> 150 us
  other arithmetic: 114 us -> 131 us
  local copies, waits for them, and re-layouts: 13.3 us -> 20.7 us
  matrix products: 16.1 us -> 19.9 us
    all_gather x0 -> x1, waiting for transfers between devices: none -> 79.7 us  [body(): terms = lax.all_gather(x, 'freq', axis=0, tiled=False)]
    psum x1 -> x0, waiting for transfers between devices: 59.4 us -> none  [body(): total = lax.psum(jnp.dot(left, right.T, precision=HIGH), 'freq')]
    another operation x10, other arithmetic: 67.8 us -> 75.2 us  [body(): factors = jnp.linalg.cholesky(jnp.stack([gram, node_gram]))]
    reduce_sum x0 -> x1, other arithmetic: none -> 4.49 us  [body(): total = terms.sum(axis=0)]
    another operation x4, other arithmetic: 40.3 us -> 43.9 us  [body(): inverses = jax.scipy.linalg.solve_triangular(factors, eye, lower=True)]
  transfers between devices with their start and end apart: 2 -> 2, of which waited for: 2 -> 2; matrix products, arithmetic and copies ran while one was open for 0% -> 1% of each run, Pallas kernels for 0% -> 0%
where the time goes in v1:
time: 337 us; the launch traced here: 336 us
  waiting for transfers between devices  150 us (45%)
  other arithmetic  131 us (39%)
  local copies, waits for them, and re-layouts  20.7 us (6%)
  matrix products  19.9 us (6%)
  between operations  14.2 us (4%)
    all_gather x1, waiting for transfers between devices, body(): terms = lax.all_gather(x, 'freq', axis=0, tiled=False)  79.7 us
    another operation x10, other arithmetic, body(): factors = jnp.linalg.cholesky(jnp.stack([gram, node_gram]))  75.2 us
    psum x1, waiting for transfers between devices, body(): pivot_rows = lax.psum(picked, 'wave')  70.8 us
    another operation x4, other arithmetic, body(): inverses = jax.scipy.linalg.solve_triangular(factors, eye, lower=True)  43.9 us
    another operation x6, local copies, waits for them, and re-layouts  7.18 us
  transfers between devices with their start and end apart: 2, of which 2 were waited for; matrix products, arithmetic and copies ran while one was open for 1% of the time, Pallas kernels for 0%

profile of v1, /device:TPU:0, one launch (start us, length us, event | category | flops | bytes accessed | tf_op | source)
XLA Modules:
  0.0 336.1 jit_solution(15563432875812331794)
XLA Ops:
  8.6 4.0 %gather_fusion = f32[256,2048]{1,0:T(8,128)S(1)} fusion(f32[256,2048]{1,0:T(8,128)} %param.3, s32[1024]{0:T(1024)S(1)} %pad_clamp_fusion), kind=kCustom, calls=%fused_computation | custom fusion | bytes 4195328 | tf_op jit(solution)/shard_map/jit(_take)/gather | solution.py:17
  12.6 1.6 select_multiply_fusion
  14.9 0.9 convert_reduce_fusion
  15.8 70.8 %all-reduce.3.cloned.1.call-done = f32[256,2048]{1,0:T(8,128)} async-done(((f32[256,2048]{1,0:T(8,128)}), f32[256,2048]{1,0:T(8,128)}) %all-reduce.3.cloned.1.call-update) | async-done | bytes 2097168 | tf_op jit(solution)/shard_map/psum | solution.py:18
  86.6 2.0 broadcast_multiply_fusion
  88.8 4.6 %fusion = f32[512,512]{1,0:T(8,128)} fusion(f32[256,2048]{1,0:T(8,128)S(1)} %copy-done.1, f32[256,2048]{1,0:T(8,128)S(1)} %copy-done, f32[256,2048]{1,0:T(8,128)S(1)} %broadcast_multiply_fusion), kind=kOutput, calls=%fused_computation.6 | convolution fusion | flops 3223322624 | bytes 7340032 | tf_op jit(solution)/shard_map/dot_general | solution.py:24
  95.9 79.7 %all-gather.3.cloned.1.call-done = f32[4096,512]{1,0:T(8,128)} async-done(((f32[512,512]{1,0:T(8,128)}), f32[4096,512]{1,0:T(8,128)}) %all-gather.3.cloned.1.call-update) | async-done | bytes 8388624 | tf_op jit(solution)/shard_map/all_gather | solution.py:25
  175.6 4.5 %reduce_sum.19 = f32[512,512]{1,0:T(8,128)S(1)} reduce(f32[8,512,512]{2,1,0:T(8,128)} %bitcast.59, f32[]{:T(128)} %constant.114.clone.1), dimensions={0}, to_apply=%region_2.3 | reduce | flops 1835008 | bytes 9437188 | tf_op jit(solution)/shard_map/reduce_sum | solution.py:26
  180.9 1.1 copy.33
  182.0 1.8 copy.34
  183.8 1.8 pad_maximum_fusion.4
  185.6 2.0 copy.22
  187.6 1.2 fusion.3
  189.6 23.6 %custom-call.17 = f32[2,128,128]{2,1,0:T(8,128)S(1)} custom-call(f32[2,128,128]{2,1,0:T(8,128)S(1)} %cholesky.122), custom_call_target="Cholesky" | custom-call | tf_op jit(solution)/shard_map/jit(cholesky)/cholesky | solution.py:29
  213.2 0.8 cholesky.117
  214.0 1.4 select_bitcast_fusion
  215.4 21.1 %custom-call.18 = f32[2,1,128,128]{2,3,1,0:T(8,128)} custom-call(f32[2,1,128,128]{3,2,1,0:T(8,128)} %select_bitcast_fusion), custom_call_target="InvertDiagBlocksLowerTriangular" | custom-call | tf_op jit(solution)/shard_map/jit(cholesky)/cholesky | solution.py:29
  236.6 1.9 constant_dynamic-update-slice_fusion.1
  238.5 2.0 convolution_subtract_fusion.2
  240.4 24.9 %custom-call.19 = f32[2,128,128]{2,1,0:T(8,128)} custom-call(f32[2,128,128]{2,1,0:T(8,128)} %convolution_subtract_fusion.2), custom_call_target="Cholesky" | custom-call | tf_op jit(solution)/shard_map/jit(cholesky)/cholesky | solution.py:29
  265.3 1.6 select_reduce_fusion
  267.1 2.0 select_select_fusion
  269.7 7.2 %while.1 = (s32[]{:T(128)}, f32[2,256,256]{2,1,0:T(8,128)}, s32[2,2]{1,0:T(2,128)S(1)}, f32[2,2,128,128]{3,2,0,1:T(8,128)}, s32[]{:T(128)}) while((s32[]{:T(128)}, f32[2,256,256]{2,1,0:T(8,128)}, s32[2,2]{1,0:T(2,128)S(1)}, f32[2,2,128,128]{3,2,0,1:T(8,128)}, s32[]{:T(128)}) %tuple.30), condition=%wide.while_cond, body=%wide.while_body.sunk | while | flops 2 | bytes 263777 | solution.py:31
  270.3 3.0 bitcast_dynamic-update-slice_fusion.2
  273.9 3.0 bitcast_dynamic-update-slice_fusion.2
  276.9 40.8 %custom-call.20 = f32[2,2,128,128]{2,3,1,0:T(8,128)} custom-call(f32[2,2,128,128]{3,2,1,0:T(8,128)} %bitcast.66), custom_call_target="InvertDiagBlocksLowerTriangular" | custom-call | tf_op jit(solution)/shard_map/jit(_solve_triangular)/vmap()/triangular_solve | solution.py:31
  317.6 1.3 fusion.14
  319.0 1.3 convolution_subtract_fusion.1
  320.3 1.5 fusion.13
  323.0 1.2 fusion.22
  324.2 2.5 convolution_subtract_fusion
  326.7 2.5 fusion.34
  (42 shorter events, 9.7 us)
Async XLA Ops:
  7.2 79.4 %all-reduce.3.cloned.1.call-start = ((), (), s32[]{:S(2)}) async-start(), calls=%async_computation | async-start | bytes 4194304 | tf_op jit(solution)/shard_map/psum | solution.py:18
  14.2 0.7 copy-start.6
  14.2 161.4 %all-gather.3.cloned.1.call-start = ((), (), s32[]{:S(2)}) async-start(), calls=%async_computation.1 | async-start | bytes 9437184 | tf_op jit(solution)/shard_map/all_gather | solution.py:25
  15.8 72.8 %copy-start = (f32[256,2048]{1,0:T(8,128)S(1)}, f32[256,2048]{1,0:T(8,128)}, u32[]{:S(2)}) copy-start(f32[256,2048]{1,0:T(8,128)} %param.3) | copy-start | bytes 6291460
  86.6 2.2 copy-start.1
  188.8 0.8 copy-start.4
  215.4 102.2 %copy-start.5 = (f32[128,256]{1,0:T(8,128)S(1)}, f32[128,256]{1,0:T(8,128)}, u32[]{:S(2)}) copy-start(f32[128,256]{1,0:T(8,128)} %get-tuple-element.28) | copy-start | bytes 393220
  320.3 2.7 copy-start.2
  324.2 2.5 copy-start.3
Sparse Core Ops, SparseCore 0:
  14.3 72.1 all-reduce.2
  93.5 82.0 all-gather.2
